TPU v7x, 32 devices: a whole 2x2x4 slice. The times are simulated.
32 devices in a mesh: dp: 2 (over x), vocab: 16 (over z, y, core).
Axes of the slice: x: 2, y: 2, z: 4, core: 2. Of those that a mesh axis runs over, the one named last changes fastest.
Arguments:
- hidden: bfloat16 [96, 8192], P('dp', 'vocab'), may hold values from -90 to 90
- weight: bfloat16 [8192, 38016], P('dp', 'vocab'), may hold values from -0.1875 to 0.1875
- targets: int32 [96], P('dp'), may hold values from 0 to 38015
- pad_mask: int32 [96], P('dp'), may hold values from 0 to 1
Outputs:
- token_nll: float32 [96], P('dp')
- nll_total: float32 [], replicated
All inputs are finite; a program needn't handle non-finite values.
Results may differ from a plain program's by a relative error of at most 0.0003.
Values may be sent and summed in bfloat16 or wider, within the bound.
No kernel may reach another device: no remote copies, remote signals or barrier semaphores. Data moves between devices by JAX's collectives and lax.ppermute only.
A program may use at most 64 MiB of HBM per device.

v0:
```python
import jax
import jax.numpy as jnp
from jax import lax
from jax.sharding import PartitionSpec as P


def merged_2(value, axis, join):
    pieces = jax.tree.map(lambda part: lax.all_gather(part, axis), value)
    head = jax.tree.map(lambda part: part[0], pieces)
    tail = jax.tree.map(lambda part: part[1:], pieces)
    subtotal, _ = lax.scan(lambda subtotal, share: (join(subtotal, share), None), head, tail)
    return subtotal


def join_stats(earlier, later):
    max_one, sum_one, pick_one = earlier
    max_two, sum_two, pick_two = later
    merged = jnp.maximum(max_one, max_two)
    return (
        merged,
        sum_one * jnp.exp(max_one - merged) + sum_two * jnp.exp(max_two - merged),
        pick_one + pick_two,
    )


def per_device(hidden, weight, targets, pad_mask):
    dp_size = lax.axis_size("dp")
    whole_width = lax.all_gather(hidden, "vocab", axis=1, tiled=True)
    tok_dev = whole_width.shape[0]
    n_cols = weight.shape[1]
    spread = lax.all_to_all(whole_width, "dp", split_axis=1, concat_axis=0, tiled=True)
    cols_sub = n_cols // dp_size
    logits = lax.psum_scatter(
        lax.dot_general(
            weight, spread, (((0,), (1,)), ((), ())), preferred_element_type=jnp.float32
        ),
        "dp",
        scatter_dimension=0,
        tiled=True,
    )
    all_targets, all_mask = (
        lax.all_gather(targets, "dp", axis=0, tiled=True),
        lax.all_gather(pad_mask, "dp", axis=0, tiled=True),
    )
    col_base = lax.axis_index("vocab") * n_cols + lax.axis_index("dp") * cols_sub
    column_ids = lax.broadcasted_iota(jnp.int32, (cols_sub, 1), 0) + col_base
    is_target = column_ids == all_targets[None, :]
    local_pick = jnp.sum(jnp.where(is_target, logits, 0.0), axis=0)
    local_max = jnp.max(logits, axis=0)
    local_sum = jnp.sum(jnp.exp(logits - local_max[None, :]), axis=0)
    row_max, exp_sum, picked = merged_2(
        (local_max, local_sum, local_pick), ("dp", "vocab"), join_stats
    )
    every_nll = all_mask.astype(jnp.float32) * (row_max + jnp.log(exp_sum) - picked)
    nll_total = jnp.sum(every_nll)
    token_nll = lax.dynamic_slice_in_dim(every_nll, lax.axis_index("dp") * tok_dev, tok_dev, 0)
    return (token_nll, nll_total)


def solution(mesh):
    placed = (P("dp", "vocab"), P("dp", "vocab"), P("dp"), P("dp"))
    return jax.shard_map(
        per_device, mesh=mesh, in_specs=placed, out_specs=(P("dp"), P()), check_vma=False
    )
```

profile of v0, /device:TPU:0, one launch (start us, length us, event | category | flops | bytes accessed | tf_op | source)
XLA Modules:
  0.0 145.3 jit_solution(8605927002165873996)
XLA Ops:
  7.2 0.0 copy-start
  7.2 0.0 copy-start.1
  7.2 0.0 copy-start.2
  7.2 0.0 all-reduce.10.cloned.1.call-start
  7.2 25.7 %all_gather.28 = bf16[48,8192]{1,0:T(8,128)(2,1)S(1)} all-gather(bf16[48,512]{1,0:T(8,128)(2,1)} %param.6), channel_id=1, replica_groups=mesh['dp'=2,'vocab'=16] {'vocab'}, dimensions={1}, use_global_device_ids=true | all-gather | bytes 835584 | tf_op jit(solution)/shard_map/all_gather | solution.py:28
  33.0 0.1 copy.12
  33.0 14.0 %all_to_all.19 = bf16[48,2,4096]{2,0,1:T(8,128)(2,1)S(1)} all-to-all(bf16[48,2,4096]{2,0,1:T(8,128)(2,1)S(1)} %bitcast.33), channel_id=1, replica_groups=mesh['dp'=2,'vocab'=16] {'dp'}, dimensions={1} | all-to-all | bytes 1572864 | tf_op jit(solution)/shard_map/all_to_all | solution.py:31
  47.0 11.1 %fusion.10 = f32[2376,96]{0,1:T(8,128)} fusion(bf16[4096,2376]{0,1:T(8,128)(2,1)} %param.7, bf16[96,4096]{1,0:T(8,128)(2,1)S(1)} %bitcast.32), kind=kOutput, calls=%fused_computation.18 | convolution fusion | flops 1868562432 | bytes 21163008 | tf_op jit(solution)/shard_map/dot_general | solution.py:34
  58.2 0.0 all-reduce.10.cloned.1.call-update
  58.2 0.0 copy-done
  58.2 0.7 fusion.9
  59.6 0.0 copy-done.1
  59.6 0.2 dynamic-update-slice
  59.8 0.0 copy-done.2
  59.8 0.2 dynamic-update-slice.3
  60.7 4.5 %all-reduce.6 = (s32[96]{0:T(128)S(1)}, s32[96]{0:T(128)S(1)}) all-reduce(s32[96]{0:T(128)S(1)} %dynamic-update-slice.3, s32[96]{0:T(128)S(1)} %dynamic-update-slice), channel_id=1, replica_groups=mesh['dp'=2,'vocab'=16] {'dp'}, use_global_device_ids=true, to_apply=%add.3 | all-reduce | flops 192 | bytes 1536
  65.2 26.8 %all-reduce.10.cloned.1.call-done = f32[2376,96]{0,1:T(8,128)} async-done(((f32[2376,96]{0,1:T(8,128)}), f32[2376,96]{0,1:T(8,128)}) %all-reduce.10.cloned.1.call-update) | async-done | bytes 912400
  92.0 1.3 dynamic-slice_reduce_fusion
  93.4 0.3 dynamic-update-slice.1
  93.7 1.4 select_reduce_fusion
  95.1 0.3 dynamic-update-slice.4
  95.3 0.3 dynamic-update-slice.2
  95.6 39.9 %all-reduce.7 = (f32[3072]{0:T(1024)S(1)}, f32[3072]{0:T(1024)S(1)}, f32[3072]{0:T(1024)S(1)}) all-reduce(f32[3072]{0:T(1024)S(1)} %dynamic-update-slice.1, f32[3072]{0:T(1024)S(1)} %dynamic-update-slice.2, f32[3072]{0:T(1024)S(1)} %dynamic-update-slice.4), channel_id=2, replica_groups=mesh['dp'=2,'vocab'=16] {'dp','vocab'}, use_global_device_ids=true, to_apply=%add.1 | all-reduce | flops 9216 | bytes 73728
  135.5 0.1 slice.33
  135.6 0.1 slice.34
  135.6 0.1 slice.35
  135.7 0.1 reshape.23
  135.8 0.1 reshape.24
  135.9 0.1 reshape.25
  135.9 1.4 while.14
  137.3 0.6 fusion.8
  137.9 0.6 dynamic_slice.13
  (40 shorter events, 1.0 us)
Async XLA Ops:
  7.2 51.1 %copy-start = (u32[32]{0:T(128)S(1)}, u32[32]{0:T(128)}, u32[]{:S(2)}) copy-start(u32[32]{0:T(128)} %constant.35) | copy-start | bytes 388
  7.2 52.4 %copy-start.1 = (s32[48]{0:T(128)S(1)}, s32[48]{0:T(128)}, u32[]{:S(2)}) copy-start(s32[48]{0:T(128)} %param.9) | copy-start | bytes 580
  7.2 52.6 %copy-start.2 = (s32[48]{0:T(128)S(1)}, s32[48]{0:T(128)}, u32[]{:S(2)}) copy-start(s32[48]{0:T(128)} %param.8) | copy-start | bytes 580
  7.2 84.8 %all-reduce.10.cloned.1.call-start = ((), (), s32[]{:S(2)}) async-start(), calls=%async_computation.1 | async-start | bytes 1867776
Sparse Core Ops, SparseCore 0:
  58.3 33.6 all-reduce.9
where the time goes:
time: 146 us; the launch traced here: 145 us
  blocking collectives  84.1 us (58%)
  waiting for transfers between devices  26.8 us (18%)
  between operations  15.5 us (11%)
  matrix products  11.1 us (8%)
  other arithmetic  4.28 us (3%)
  local copies, waits for them, and re-layouts  3.04 us (2%)
    unnamed x2, blocking collectives  44.4 us
    unnamed x2, waiting for transfers between devices  26.8 us
    all_gather x1, blocking collectives, per_device(): whole_width = lax.all_gather(hidden, 'vocab', axis=1, tiled=True)  25.7 us
    all_to_all x1, blocking collectives, per_device(): lax.all_to_all(whole_width, 'dp', split_axis=1, concat_axis=0, tiled=True)  14 us
    dot_general x1, matrix products, per_device(): lax.dot_general(weight, spread, (((0,), (1,)), ((), ())), preferred_eleme...  11.1 us
  transfers between devices with their start and end apart: 1, of which 1 were waited for; matrix products, arithmetic and copies ran while one was open for 1% of the time, Pallas kernels for 0%

commit v1 on v0

--- a/solution.py
+++ b/solution.py
@@ -28,7 +28,10 @@
     whole_width = lax.all_gather(hidden, "vocab", axis=1, tiled=True)
     tok_dev = whole_width.shape[0]
     n_cols = weight.shape[1]
-    spread = lax.all_to_all(whole_width, "dp", split_axis=1, concat_axis=0, tiled=True)
+    spread = jnp.concatenate(
+        lax.all_to_all(jnp.stack(jnp.split(whole_width, lax.axis_size("dp"), axis=1)), "dp", 0, 0),
+        axis=0,
+    )
     cols_sub = n_cols // dp_size
     logits = lax.psum_scatter(
         lax.dot_general(

time: 146 us -> 148 us (1.014)
  matrix products: 11.1 us -> 13.6 us
    dot_general x1, matrix products: 11.1 us -> 13.6 us  [per_device(): lax.dot_general(weight, spread, (((0,), (1,)), ((), ())), preferred_eleme...]
where the time goes in v1:
time: 148 us
  blocking collectives  84.1 us (57%)
  waiting for transfers between devices  26.8 us (18%)
  between operations  15.5 us (10%)
  matrix products  13.6 us (9%)
  other arithmetic  4.35 us (3%)
  local copies, waits for them, and re-layouts  3.04 us (2%)
    unnamed x2, blocking collectives  44.4 us
    unnamed x2, waiting for transfers between devices  26.8 us
    all_gather x1, blocking collectives, per_device(): whole_width = lax.all_gather(hidden, 'vocab', axis=1, tiled=True)  25.7 us
    all_to_all x1, blocking collectives, per_device(): lax.all_to_all(jnp.stack(jnp.split(whole_width, lax.axis_size('dp'), axis...  14 us
    dot_general x1, matrix products, per_device(): lax.dot_general(weight, spread, (((0,), (1,)), ((), ())), preferred_eleme...  13.6 us
  transfers between devices with their start and end apart: 1, of which 1 were waited for; matrix products, arithmetic and copies ran while one was open for 1% of the time, Pallas kernels for 0%

profile of v1, /device:TPU:0, one launch (start us, length us, event | category | flops | bytes accessed | tf_op | source)
XLA Modules:
  0.0 147.9 jit_solution(5381424502799600877)
XLA Ops:
  7.2 0.0 copy-start
  7.2 0.0 copy-start.1
  7.2 0.0 copy-start.2
  7.2 0.0 all-reduce.10.cloned.1.call-start
  7.2 25.7 %all_gather.28 = bf16[48,8192]{1,0:T(8,128)(2,1)S(1)} all-gather(bf16[48,512]{1,0:T(8,128)(2,1)} %param.6), channel_id=1, replica_groups=mesh['dp'=2,'vocab'=16] {'vocab'}, dimensions={1}, use_global_device_ids=true | all-gather | bytes 835584 | tf_op jit(solution)/shard_map/all_gather | solution.py:28
  33.0 0.1 slice_bitcast_fusion.1
  33.0 0.1 pad_maximum_fusion
  33.1 14.0 %all_to_all.5 = bf16[2,48,4096]{2,1,0:T(8,128)(2,1)S(1)} all-to-all(bf16[2,48,4096]{2,1,0:T(8,128)(2,1)S(1)} %pad_maximum_fusion), channel_id=1, replica_groups=mesh['dp'=2,'vocab'=16] {'dp'}, dimensions={0} | all-to-all | bytes 1572864 | tf_op jit(solution)/shard_map/all_to_all | solution.py:32
  47.1 13.6 %convolution_bitcast_fusion = f32[2376,96]{0,1:T(8,128)} fusion(bf16[96,4096]{1,0:T(8,128)(2,1)S(1)} %bitcast.32, bf16[4096,2376]{0,1:T(8,128)(2,1)} %param.7), kind=kOutput, calls=%fused_computation.10 | convolution fusion | flops 1868562432 | bytes 21163008 | tf_op jit(solution)/shard_map/dot_general | solution.py:37
  60.7 0.0 all-reduce.10.cloned.1.call-update
  60.7 0.0 copy-done
  60.7 0.7 fusion.9
  62.1 0.0 copy-done.1
  62.1 0.2 dynamic-update-slice
  62.3 0.2 dynamic-update-slice.3
  63.3 4.5 %all-reduce.6 = (s32[96]{0:T(128)S(1)}, s32[96]{0:T(128)S(1)}) all-reduce(s32[96]{0:T(128)S(1)} %dynamic-update-slice.3, s32[96]{0:T(128)S(1)} %dynamic-update-slice), channel_id=1, replica_groups=mesh['dp'=2,'vocab'=16] {'dp'}, use_global_device_ids=true, to_apply=%add.3 | all-reduce | flops 192 | bytes 1536
  67.7 26.8 %all-reduce.10.cloned.1.call-done = f32[2376,96]{0,1:T(8,128)} async-done(((f32[2376,96]{0,1:T(8,128)}), f32[2376,96]{0,1:T(8,128)}) %all-reduce.10.cloned.1.call-update) | async-done | bytes 912400
  94.5 1.3 dynamic-slice_reduce_fusion
  95.9 0.3 dynamic-update-slice.1
  96.2 1.4 select_reduce_fusion
  97.6 0.3 dynamic-update-slice.4
  97.8 0.3 dynamic-update-slice.2
  98.1 39.9 %all-reduce.7 = (f32[3072]{0:T(1024)S(1)}, f32[3072]{0:T(1024)S(1)}, f32[3072]{0:T(1024)S(1)}) all-reduce(f32[3072]{0:T(1024)S(1)} %dynamic-update-slice.1, f32[3072]{0:T(1024)S(1)} %dynamic-update-slice.2, f32[3072]{0:T(1024)S(1)} %dynamic-update-slice.4), channel_id=2, replica_groups=mesh['dp'=2,'vocab'=16] {'dp','vocab'}, use_global_device_ids=true, to_apply=%add.1 | all-reduce | flops 9216 | bytes 73728
  138.0 0.1 slice.33
  138.1 0.1 slice.34
  138.2 0.1 slice.35
  138.2 0.1 reshape.24
  138.3 0.1 reshape.25
  138.4 0.1 reshape.26
  138.4 1.4 while.14
  139.8 0.6 fusion.8
  140.4 0.6 dynamic_slice.13
  (41 shorter events, 1.0 us)
Async XLA Ops:
  7.2 53.6 %copy-start = (u32[32]{0:T(128)S(1)}, u32[32]{0:T(128)}, u32[]{:S(2)}) copy-start(u32[32]{0:T(128)} %constant.35) | copy-start | bytes 388
  7.2 54.9 %copy-start.1 = (s32[48]{0:T(128)S(1)}, s32[48]{0:T(128)}, u32[]{:S(2)}) copy-start(s32[48]{0:T(128)} %param.9) | copy-start | bytes 580
  7.2 55.1 %copy-start.2 = (s32[48]{0:T(128)S(1)}, s32[48]{0:T(128)}, u32[]{:S(2)}) copy-start(s32[48]{0:T(128)} %param.8) | copy-start | bytes 580
  7.2 87.3 %all-reduce.10.cloned.1.call-start = ((), (), s32[]{:S(2)}) async-start(), calls=%async_computation.1 | async-start | bytes 1867776
Sparse Core Ops, SparseCore 0:
  60.8 33.6 all-reduce.9
